TPU v7x, 32 devices: a whole 2x2x4 slice. The times are simulated.
32 devices in a mesh: expert: 4 (over x, core), shard: 8 (over z, y).
Axes of the slice: x: 2, y: 2, z: 4, core: 2. Of those that a mesh axis runs over, the one named last changes fastest.
Arguments:
- train_down: float32 [16, 6400, 4096], P('expert', None, 'shard'), may hold values from -0.109375 to 0.109375
- other_down: bfloat16 [16, 6400, 4096], P('expert', None, 'shard'), may hold values from -0.0390625 to 0.0390625
- router_weight: float32 [4096, 16], P('shard', 'expert'), may hold values from -0.09375 to 0.09375
- router_gain: float32 [4096], P('shard'), may hold values from 0.25 to 1.75
Outputs:
- ready_down: bfloat16 [16, 6400, 4096], P('expert', 'shard')
- scale_down: float32 [16, 6400], P('expert', 'shard')
- serve_router: bfloat16 [4096, 16], replicated
All inputs are finite; a program needn't handle non-finite values. Where the computation divides by a largest or mean magnitude, that divisor is 1e-20 or more.
Results may differ from a plain program's by a relative error of at most 0.001.
Values may be sent and summed in bfloat16 or wider, within the bound.
A program may use at most 256 MiB of HBM per device.

v0:
```python
import jax
import jax.numpy as jnp
from jax import lax
from jax.sharding import PartitionSpec as P


def per_device(train_down, other_down, router_weight, router_gain):
    latest_down = train_down + other_down.astype(jnp.float32)
    scale_down = lax.pmax(jnp.max(jnp.abs(latest_down), axis=2), "shard")
    narrow_down = (latest_down / jnp.expand_dims(scale_down, 2)).astype(jnp.bfloat16)
    ready_down = lax.all_to_all(narrow_down, "shard", split_axis=1, concat_axis=2, tiled=True)
    scale_down = lax.dynamic_slice_in_dim(
        scale_down, lax.axis_index("shard") * ready_down.shape[1], ready_down.shape[1], axis=1
    )
    part_router = (router_weight * router_gain[:, None]).astype(jnp.bfloat16)
    row_router = lax.all_gather(part_router, "shard", axis=0, tiled=True)
    serve_router = lax.all_gather(row_router, "expert", axis=1, tiled=True)
    return (ready_down, scale_down, serve_router)


def solution(mesh):
    in_specs = (
        P("expert", None, "shard"),
        P("expert", None, "shard"),
        P("shard", "expert"),
        P("shard"),
    )
    out_specs = (P("expert", "shard", None), P("expert", "shard"), P())
    return jax.shard_map(
        per_device, mesh=mesh, in_specs=in_specs, out_specs=out_specs, check_vma=False
    )
```

profile of v0, /device:TPU:0, one launch (start us, length us, event | category | flops | bytes accessed | tf_op | source)
XLA Modules:
  0.0 903.4 jit_solution(8712372053355540380)
XLA Ops:
  7.2 0.0 all-reduce.2.cloned.1.call-start
  7.2 24.2 %abs_reduce_fusion = f32[4,6400]{1,0:T(4,128)S(1)} fusion(f32[4,6400,512]{2,1,0:T(8,128)} %param.4, bf16[4,6400,512]{2,1,0:T(8,128)(2,1)} %param.5), kind=kLoop, calls=%fused_computation.1 | loop fusion | flops 52403200 | bytes 78745600 | tf_op jit(solution)/shard_map/reduce_max | solution.py:9
  31.4 2.3 copy.21
  33.7 0.0 all-reduce.2.cloned.1.call-update
  33.7 135.6 %all-reduce.2.cloned.1.call-done = f32[4,6400]{0,1:T(8,128)} async-done(((f32[4,6400]{0,1:T(8,128)}), f32[4,6400]{0,1:T(8,128)}) %all-reduce.2.cloned.1.call-update) | async-done | bytes 102416 | tf_op jit(solution)/shard_map/pmax | solution.py:9
  169.4 2.4 copy.17
  171.8 34.3 %divide_convert_fusion = bf16[4,6400,512]{2,1,0:T(8,128)(2,1)} fusion(f32[4,6400,512]{2,1,0:T(8,128)} %param.4, bf16[4,6400,512]{2,1,0:T(8,128)(2,1)} %param.5, f32[4,6400]{1,0:T(4,128)S(1)} %copy.17), kind=kLoop, calls=%fused_computation | loop fusion | flops 52428800 | bytes 104960000 | tf_op jit(solution)/shard_map/convert_element_type | solution.py:10
  206.1 33.4 %copy.18 = bf16[4,6400,512]{2,0,1:T(4,128)(2,1)} copy(bf16[4,6400,512]{2,1,0:T(8,128)(2,1)} %divide_convert_fusion) | data formatting | bytes 52428800 | tf_op jit(solution)/shard_map/convert_element_type | solution.py:10
  239.5 0.0 copy-start
  239.5 0.0 copy-start.1
  239.5 6.6 all-to-all-start
  246.1 0.0 copy-done
  246.2 0.0 copy-done.1
  246.2 585.0 %all_gather.6 = bf16[4096,4]{0,1:T(4,128)(2,1)S(1)} all-gather(bf16[512,4]{0,1:T(4,128)(2,1)S(1)} %multiply_convert_fusion), channel_id=1, replica_groups=mesh['expert'=4,'shard'=8] {'shard'}, dimensions={0}, use_global_device_ids=true | all-gather | bytes 36864 | tf_op jit(solution)/shard_map/all_gather | solution.py:16
  831.2 5.4 all-gather
  836.6 0.7 reshape.9
  837.3 1.0 constant_dynamic-slice_fusion
  838.4 0.8 copy.20
  839.1 0.0 all-to-all-done
  839.1 18.2 %copy.19 = bf16[4,800,8,512]{3,2,1,0:T(8,128)(2,1)} copy(bf16[4,800,8,512]{3,0,1,2:T(4,128)(2,1)} %bitcast.1) | data formatting | bytes 52428800 | tf_op jit(solution)/shard_map/all_to_all | solution.py:11
  857.4 39.2 %all_to_all.16 = bf16[4,800,4096]{2,1,0:T(8,128)(2,1)} reshape(bf16[4,800,8,512]{3,2,1,0:T(8,128)(2,1)} %copy.19) | data formatting | bytes 52428800 | tf_op jit(solution)/shard_map/all_to_all | solution.py:11
  (1 shorter events, 0.0 us)
Async XLA Ops:
  7.2 162.2 %all-reduce.2.cloned.1.call-start = ((), (), s32[]{:S(2)}) async-start(), calls=%async_computation.1 | async-start | bytes 6553600 | tf_op jit(solution)/shard_map/pmax | solution.py:9
  239.5 6.7 copy-start
  239.5 6.7 copy-start.1
  239.5 599.6 %all-to-all-start = ((bf16[4,6400,512]{2,0,1:T(4,128)(2,1)}), bf16[4,6400,512]{2,0,1:T(4,128)(2,1)}, u32[]{:S(2)}, u32[]{:S(2)}) async-start(bf16[4,6400,512]{2,0,1:T(4,128)(2,1)} %copy.18), calls=%async_computation | async-start | bytes 52428800 | tf_op jit(solution)/shard_map/all_to_all | solution.py:11
Sparse Core Ops, SparseCore 0:
  33.9 135.4 all-reduce.1
where the time goes:
time: 905 us; the launch traced here: 903 us
  blocking collectives  590 us (65%)
  waiting for transfers between devices  136 us (15%)
  local copies, waits for them, and re-layouts  98 us (11%)
  other arithmetic  58.5 us (6%)
  between operations  14.1 us (2%)
    all_gather x1, blocking collectives, per_device(): row_router = lax.all_gather(part_router, 'shard', axis=0, tiled=True)  585 us
    pmax x1, waiting for transfers between devices, per_device(): scale_down = lax.pmax(jnp.max(jnp.abs(latest_down), axis=2), 'shard')  136 us
    all_to_all x2, local copies, waits for them, and re-layouts, per_device(): lax.all_to_all(narrow_down, 'shard', split_axis=1, concat_axis=2, tiled=T...  57.4 us
    convert_element_type x1, other arithmetic, per_device(): (latest_down / jnp.expand_dims(scale_down, 2)).astype(jnp.bfloat16)  34.3 us
    convert_element_type x1, local copies, waits for them, and re-layouts, per_device(): (latest_down / jnp.expand_dims(scale_down, 2)).astype(jnp.bfloat16)  33.4 us
    reduce_max x1, other arithmetic, per_device(): scale_down = lax.pmax(jnp.max(jnp.abs(latest_down), axis=2), 'shard')  24.2 us
  transfers between devices with their start and end apart: 2, of which 1 were waited for; matrix products, arithmetic and copies ran while one was open for 0% of the time, Pallas kernels for 0%

commit v1 on v0

--- a/solution.py
+++ b/solution.py
@@ -4,11 +4,20 @@
 from jax.sharding import PartitionSpec as P
 
 
+def divide_sites(target, lane_axis):
+    reached = lax.axis_size(lane_axis)
+    spare = jnp.split(target, reached, 1)
+    v_next = jnp.stack(spare)
+    reply = lax.all_to_all(v_next, lane_axis, 0, 0)
+    local_out = jnp.concatenate(reply, 2)
+    return local_out
+
+
 def per_device(train_down, other_down, router_weight, router_gain):
     latest_down = train_down + other_down.astype(jnp.float32)
     scale_down = lax.pmax(jnp.max(jnp.abs(latest_down), axis=2), "shard")
     narrow_down = (latest_down / jnp.expand_dims(scale_down, 2)).astype(jnp.bfloat16)
-    ready_down = lax.all_to_all(narrow_down, "shard", split_axis=1, concat_axis=2, tiled=True)
+    ready_down = divide_sites(narrow_down, "shard")
     scale_down = lax.dynamic_slice_in_dim(
         scale_down, lax.axis_index("shard") * ready_down.shape[1], ready_down.shape[1], axis=1
     )

time: 905 us -> 792 us (0.88)
  waiting for transfers between devices: 136 us -> 72.5 us
  local copies, waits for them, and re-layouts: 98 us -> 50.6 us
    pmax x1, waiting for transfers between devices: 136 us -> 72.5 us  [per_device(): scale_down = lax.pmax(jnp.max(jnp.abs(latest_down), axis=2), 'shard')]
    all_to_all x2 -> x0, local copies, waits for them, and re-layouts: 57.4 us -> none  [per_device(): lax.all_to_all(narrow_down, 'shard', split_axis=1, concat_axis=2, tiled=T...]
    convert_element_type x1 -> x0, local copies, waits for them, and re-layouts: 33.4 us -> none  [per_device(): (latest_down / jnp.expand_dims(scale_down, 2)).astype(jnp.bfloat16)]
    unnamed x7 -> x12, local copies, waits for them, and re-layouts: 3.75 us -> 27.5 us
    reshape x0 -> x1, local copies, waits for them, and re-layouts: none -> 17.9 us  [divide_sites(): local_out = jnp.concatenate(reply, 2)]
where the time goes in v1:
time: 792 us
  blocking collectives  589 us (74%)
  waiting for transfers between devices  72.5 us (9%)
  other arithmetic  59.2 us (7%)
  local copies, waits for them, and re-layouts  50.6 us (6%)
  between operations  14.1 us (2%)
    all_gather x1, blocking collectives, per_device(): row_router = lax.all_gather(part_router, 'shard', axis=0, tiled=True)  583 us
    pmax x1, waiting for transfers between devices, per_device(): scale_down = lax.pmax(jnp.max(jnp.abs(latest_down), axis=2), 'shard')  72.5 us
    convert_element_type x1, other arithmetic, per_device(): (latest_down / jnp.expand_dims(scale_down, 2)).astype(jnp.bfloat16)  34.4 us
    unnamed x12, local copies, waits for them, and re-layouts  27.5 us
    reduce_max x1, other arithmetic, per_device(): scale_down = lax.pmax(jnp.max(jnp.abs(latest_down), axis=2), 'shard')  24.9 us
    reshape x1, local copies, waits for them, and re-layouts, divide_sites(): local_out = jnp.concatenate(reply, 2)  17.9 us
  transfers between devices with their start and end apart: 2, of which 1 were waited for; matrix products, arithmetic and copies ran while one was open for 0% of the time, Pallas kernels for 0%

profile of v1, /device:TPU:0, one launch (start us, length us, event | category | flops | bytes accessed | tf_op | source)
XLA Modules:
  0.0 791.9 jit_solution(10896908688259474292)
XLA Ops:
  7.2 0.0 all-reduce.2.cloned.1.call-start
  7.2 24.9 %abs_reduce_fusion = f32[4,6400]{1,0:T(4,128)} fusion(f32[4,6400,512]{2,1,0:T(8,128)} %param.4, bf16[4,6400,512]{2,1,0:T(8,128)(2,1)} %param.5), kind=kLoop, calls=%fused_computation.1 | loop fusion | flops 52403200 | bytes 78745600 | tf_op jit(solution)/shard_map/reduce_max | solution.py:18
  32.1 0.0 all-reduce.2.cloned.1.call-update
  32.1 72.5 %all-reduce.2.cloned.1.call-done = f32[4,6400]{1,0:T(4,128)} async-done(((f32[4,6400]{1,0:T(4,128)}), f32[4,6400]{1,0:T(4,128)}) %all-reduce.2.cloned.1.call-update) | async-done | bytes 102416 | tf_op jit(solution)/shard_map/pmax | solution.py:18
  104.6 34.4 %divide_convert_fusion = bf16[4,6400,512]{2,1,0:T(8,128)(2,1)} fusion(f32[4,6400,512]{2,1,0:T(8,128)} %param.4, bf16[4,6400,512]{2,1,0:T(8,128)(2,1)} %param.5, f32[4,6400]{1,0:T(4,128)} %all-reduce.2.cloned.1.call-done), kind=kLoop, calls=%fused_computation | loop fusion | flops 52428800 | bytes 104960000 | tf_op jit(solution)/shard_map/convert_element_type | solution.py:19
  139.0 3.8 fusion.7
  142.8 3.8 fusion.6
  146.6 3.8 fusion.5
  150.4 3.8 fusion.4
  154.3 3.9 fusion.3
  158.1 3.8 fusion.2
  162.0 3.8 fusion.1
  165.8 3.8 fusion
  169.6 0.0 copy-start
  169.6 0.0 copy-start.1
  169.6 6.6 all-to-all-start
  176.2 0.0 copy-done
  176.2 0.0 copy-done.1
  176.3 583.4 %all_gather.6 = bf16[4096,4]{0,1:T(4,128)(2,1)S(1)} all-gather(bf16[512,4]{0,1:T(4,128)(2,1)S(1)} %multiply_convert_fusion), channel_id=1, replica_groups=mesh['expert'=4,'shard'=8] {'shard'}, dimensions={0}, use_global_device_ids=true | all-gather | bytes 36864 | tf_op jit(solution)/shard_map/all_gather | solution.py:25
  759.7 5.4 all-gather
  765.1 0.7 reshape.17
  765.8 1.4 constant_dynamic-slice_fusion
  767.2 0.0 all-to-all-done
  767.2 17.9 %copy.9 = bf16[8,4,100,8,512]{4,3,0,2,1:T(8,128)(2,1)} copy(bf16[8,4,100,8,512]{4,3,2,1,0:T(8,128)(2,1)} %bitcast.13) | data formatting | bytes 52428800 | tf_op jit(solution)/shard_map/reshape | solution.py:12
  (1 shorter events, 0.0 us)
Async XLA Ops:
  7.2 97.4 %all-reduce.2.cloned.1.call-start = ((), (), s32[]{:S(2)}) async-start(), calls=%async_computation.1 | async-start | bytes 204800 | tf_op jit(solution)/shard_map/pmax | solution.py:18
  169.6 6.6 copy-start
  169.6 6.6 copy-start.1
  169.6 597.6 %all-to-all-start = ((bf16[8,4,800,512]{3,2,1,0:T(8,128)(2,1)}), bf16[8,4,800,512]{3,2,1,0:T(8,128)(2,1)}, u32[]{:S(2)}, u32[]{:S(2)}) async-start(bf16[8,4,800,512]{3,2,1,0:T(8,128)(2,1)} %fusion), calls=%async_computation | async-start | bytes 52428800 | tf_op jit(solution)/shard_map/all_to_all | solution.py:11
Sparse Core Ops, SparseCore 0:
  32.2 72.3 all-reduce.1
